TPU v7x, 32 devices: a whole 2x2x4 slice. The times are simulated.
32 devices in a mesh: dp: 4 (over x, core), tensor: 8 (over z, y).
Axes of the slice: x: 2, y: 2, z: 4, core: 2. Of those that a mesh axis runs over, the one named last changes fastest.
Arguments:
- attn_ctx: bfloat16 [2048, 8192], P('dp', 'tensor'), may hold values from -6 to 6
- w_out: bfloat16 [8192, 8192], P('tensor'), may hold values from -0.09375 to 0.09375
- resid: bfloat16 [2048, 8192], P(('dp', 'tensor')), may hold values from -6 to 6
- teacher_gain: bfloat16 [8192], replicated, may hold values from 0.25 to 1.75
- dest_row: int32 [2048], replicated, may hold values from 0 to 2047, as said below
- student_in: bfloat16 [2048, 4096], P('dp', 'tensor'), may hold values from -6 to 6
- student_gain: bfloat16 [4096], replicated, may hold values from 0.25 to 1.75
- w_gate: bfloat16 [4096, 14336], P('dp', 'tensor'), may hold values from -0.09375 to 0.09375
- w_up: bfloat16 [4096, 14336], P('dp', 'tensor'), may hold values from -0.09375 to 0.09375
- w_down: bfloat16 [14336, 4096], P('tensor', 'dp'), may hold values from -0.0625 to 0.0625
- proj: bfloat16 [4096, 8192], P('dp', 'tensor'), may hold values from -0.09375 to 0.09375
Outputs:
- student_out: bfloat16 [2048, 4096], P('dp', 'tensor')
- row_loss: float32 [2048], P('dp')
- residue: float32 [2048, 8192], P('dp', 'tensor')
Inputs may be any that keep to these rules, and one draw needn't show every extreme that they name: A permutation of the rows; of the 64 rows i in one aligned block of teacher rows, at most 32 have dest_row[i] in any one tile of 512 student rows, and some tile receives exactly 32 of them.
All inputs are finite; a program needn't handle non-finite values.
Results may differ from a plain program's by a relative error of at most 0.012.
Values may be sent and summed in bfloat16 or wider, within the bound.
A program may use at most 192 MiB of HBM per device.

v0:
```python
import jax
import jax.numpy as jnp
from jax import lax
from jax.sharding import PartitionSpec as P

HT = 8192


def local(
    attn_ctx,
    w_out,
    resid,
    teacher_gain,
    dest_row,
    student_in,
    student_gain,
    w_gate,
    w_up,
    w_down,
    proj,
):
    tensor_count = lax.axis_size("tensor")
    group_count = lax.axis_size("dp")
    tile_rows = attn_ctx.shape[0]
    own_rows = resid.shape[0]
    portion = attn_ctx
    summed = lax.psum_scatter(
        jnp.dot(portion, w_out, preferred_element_type=jnp.float32).astype(jnp.bfloat16),
        "tensor",
        scatter_dimension=0,
        tiled=True,
    ).astype(jnp.float32)
    teacher_hidden = resid.astype(jnp.float32) + summed
    square_mean = jnp.mean(teacher_hidden * teacher_hidden, axis=1, keepdims=True)
    teacher_final = (
        teacher_hidden * lax.rsqrt(square_mean + 1e-06) * teacher_gain.astype(jnp.float32)
    ).astype(jnp.bfloat16)
    capacity = 2 * own_rows // group_count
    source_count = group_count * tensor_count
    group_ids = (dest_row // tile_rows).reshape(source_count, own_rows)
    onehot = (group_ids[:, :, None] == jnp.arange(group_count)[None, None, :]).astype(jnp.int32)
    slot_index = jnp.sum((jnp.cumsum(onehot, 1) - onehot) * onehot, 2)
    my_source = lax.axis_index("dp") * tensor_count + lax.axis_index("tensor")
    own_groups = lax.dynamic_index_in_dim(group_ids, my_source, 0, keepdims=False)
    own_slots = lax.dynamic_index_in_dim(slot_index, my_source, 0, keepdims=False)
    target_slot = own_groups * capacity + own_slots
    selector = (target_slot[None, :] == jnp.arange(group_count * capacity)[:, None]).astype(
        jnp.bfloat16
    )
    packed = jnp.dot(selector, teacher_final, preferred_element_type=jnp.float32).astype(
        jnp.bfloat16
    )
    col_width = teacher_final.shape[1] // tensor_count
    send_blocks = packed.reshape(group_count, capacity, tensor_count, col_width).transpose(
        0, 2, 1, 3
    )
    arrived = lax.all_to_all(
        lax.all_to_all(send_blocks, "dp", split_axis=0, concat_axis=0, tiled=True),
        "tensor",
        split_axis=1,
        concat_axis=1,
        tiled=True,
    )
    flattened = arrived.reshape(source_count * capacity, col_width)
    arrival_index = (jnp.arange(source_count)[:, None] * capacity + slot_index).reshape(-1)
    inverse = jnp.zeros(dest_row.shape, jnp.int32).at[dest_row].set(arrival_index)
    own_arrivals = lax.dynamic_slice_in_dim(inverse, lax.axis_index("dp") * tile_rows, tile_rows, 0)
    target = jnp.take(flattened, own_arrivals, axis=0)
    gathered = lax.all_gather(student_in, "tensor", axis=1, tiled=True)
    x_full = gathered.astype(jnp.float32)
    student_mean = jnp.mean(x_full * x_full, axis=1, keepdims=True)
    normed = (x_full * lax.rsqrt(student_mean + 1e-05) * student_gain.astype(jnp.float32)).astype(
        jnp.bfloat16
    )

    def add_rows(portion):
        return jnp.dot(normed, portion, preferred_element_type=jnp.float32)

    gate_acts = add_rows(lax.all_gather(w_gate, "dp", axis=0, tiled=True))
    up_acts = add_rows(lax.all_gather(w_up, "dp", axis=0, tiled=True))
    hidden = (jax.nn.silu(gate_acts) * up_acts).astype(jnp.bfloat16)
    partial_sum = jnp.dot(
        hidden, lax.all_gather(w_down, "dp", axis=1, tiled=True), preferred_element_type=jnp.float32
    )
    local_cols = student_in.shape[1]
    mlp_sum = lax.psum(partial_sum.astype(jnp.bfloat16), "tensor").astype(jnp.float32)
    out_full = (x_full + mlp_sum).astype(jnp.bfloat16)
    out_local = lax.dynamic_slice_in_dim(
        out_full, lax.axis_index("tensor") * local_cols, local_cols, 1
    )
    pred = jnp.dot(
        out_full, lax.all_gather(proj, "dp", axis=0, tiled=True), preferred_element_type=jnp.float32
    )
    residue = pred - target.astype(jnp.float32)
    row_error = jnp.sum(residue * residue, axis=1)
    row_loss = lax.psum(row_error, "tensor") / HT
    return (out_local, row_loss, residue)


def solution(mesh):
    placed = (
        P("dp", "tensor"),
        P("tensor", None),
        P(("dp", "tensor"), None),
        P(),
        P(),
        P("dp", "tensor"),
        P(),
        P("dp", "tensor"),
        P("dp", "tensor"),
        P("tensor", "dp"),
        P("dp", "tensor"),
    )
    return jax.shard_map(
        local,
        mesh=mesh,
        in_specs=placed,
        out_specs=(P("dp", "tensor"), P("dp"), P("dp", "tensor")),
        check_vma=False,
    )
```

profile of v0, /device:TPU:0, one launch (start us, length us, event | category | flops | bytes accessed | tf_op | source)
XLA Modules:
  0.0 813.1 jit_solution(8429802727703756237)
XLA Ops:
  7.2 0.0 copy-start
  7.2 0.0 all-gather.6.cloned.1.call-start
  7.2 0.7 all-gather.6.cloned.1.call-update
  7.9 0.0 all-gather.8.cloned.1.call-start
  8.0 0.7 all-gather.8.cloned.1.call-update
  8.7 0.0 all-gather.12.cloned.1.call-start
  8.7 0.7 all-gather.12.cloned.1.call-update
  9.4 0.0 all-gather.10.cloned.1.call-start
  9.4 0.5 all-gather.10.cloned.1.call-update
  10.0 0.0 reduce-scatter.2.cloned.1.call-start
  10.0 0.0 copy-done
  10.0 16.8 %convolution_convert_fusion = bf16[512,8192]{1,0:T(8,128)(2,1)} fusion(bf16[512,1024]{1,0:T(8,128)(2,1)S(1)} %copy-done, bf16[1024,8192]{1,0:T(8,128)(2,1)} %param.12), kind=kOutput, calls=%fused_computation.5 | convolution fusion | flops 8594128896 | bytes 26214400 | tf_op jit(solution)/shard_map/dot_general | solution.py:28
  26.8 0.0 copy-start.6
  26.8 0.0 reduce-scatter.2.cloned.1.call-update
  26.8 0.2 all-reduce.2.cloned.1.call-start
  27.1 0.4 copy-done.6
  27.5 59.9 %all-gather.6.cloned.1.call-done = bf16[512,4096]{1,0:T(8,128)(2,1)} async-done(((bf16[512,512]{1,0:T(8,128)(2,1)}), bf16[512,4096]{1,0:T(8,128)(2,1)}) %all-gather.6.cloned.1.call-update) | async-done | bytes 4194320 | tf_op jit(solution)/shard_map/all_gather | solution.py:69
  87.4 3.1 fusion
  90.5 90.7 %all-gather.8.cloned.1.call-done = bf16[4096,1792]{1,0:T(8,128)(2,1)} async-done(((bf16[1024,1792]{1,0:T(8,128)(2,1)}), bf16[4096,1792]{1,0:T(8,128)(2,1)}) %all-gather.8.cloned.1.call-update) | async-done | bytes 14680080 | tf_op jit(solution)/shard_map/all_gather | solution.py:79
  181.2 14.7 %fusion.11 = f32[512,1792]{1,0:T(8,128)} fusion(bf16[4096,1792]{1,0:T(8,128)(2,1)} %all-gather.8.cloned.1.call-done, bf16[512,4096]{1,0:T(8,128)(2,1)} %all-gather.6.cloned.1.call-done, f32[4096]{0:T(1024)S(1)} %convert_element_type.47, f32[512]{0:T(512)S(1)} %add_rsqrt_fusion), kind=kOutput, calls=%fused_computation.23 | convolution fusion | flops 7524581376 | bytes 22562816 | tf_op jit(solution)/shard_map/dot_general | solution.py:77
  195.8 80.9 %all-gather.12.cloned.1.call-done = bf16[1792,4096]{1,0:T(8,128)(2,1)} async-done(((bf16[1792,1024]{1,0:T(8,128)(2,1)}), bf16[1792,4096]{1,0:T(8,128)(2,1)}) %all-gather.12.cloned.1.call-update) | async-done | bytes 14680080 | tf_op jit(solution)/shard_map/all_gather | solution.py:83
  276.8 95.4 %all-gather.10.cloned.1.call-done = bf16[4096,1792]{1,0:T(8,128)(2,1)} async-done(((bf16[1024,1792]{1,0:T(8,128)(2,1)}), bf16[4096,1792]{1,0:T(8,128)(2,1)}) %all-gather.10.cloned.1.call-update) | async-done | bytes 14680080 | tf_op jit(solution)/shard_map/all_gather | solution.py:80
  372.2 28.8 %convolution_convert_fusion.2 = bf16[512,4096]{1,0:T(8,128)(2,1)} fusion(bf16[1792,4096]{1,0:T(8,128)(2,1)} %all-gather.12.cloned.1.call-done, f32[512,1792]{1,0:T(8,128)} %fusion.11, bf16[4096,1792]{1,0:T(8,128)(2,1)} %all-gather.10.cloned.1.call-done, bf16[512,4096]{1,0:T(8,128)(2,1)} %all-gather.6.cloned.1.call-done, f32[4096]{0:T(1024)S(1)} %convert_element_type.47, ...), kind=kOutput, calls=%fused_computation.11 | convolution fusion | flops 15048376320 | bytes 41437184 | tf_op jit(solution)/shard_map/dot_general | solution.py:82
  401.0 0.0 copy-start.5
  401.0 0.0 copy-start.7
  401.0 0.0 copy-start.3
  401.0 0.0 all-reduce.2.cloned.1.call-update
  401.0 0.3 all-gather.14.cloned.1.call-start
  401.3 0.5 all-gather.14.cloned.1.call-update
  401.8 0.0 copy-done.5
  401.8 0.0 copy-done.7
  401.8 0.1 eq.30
  401.9 0.1 copy.29
  402.0 1.7 select_reduce_fusion
  403.7 0.2 add_reduce_fusion
  403.9 119.3 %reduce-scatter.2.cloned.1.call-done = bf16[64,8192]{1,0:T(8,128)(2,1)} async-done(((bf16[512,8192]{1,0:T(8,128)(2,1)}), bf16[64,8192]{1,0:T(8,128)(2,1)}) %reduce-scatter.2.cloned.1.call-update) | async-done | bytes 1048592 | tf_op jit(solution)/shard_map/reduce_scatter | solution.py:27
  523.2 0.0 copy-done.3
  523.2 1.7 multiply_reduce_fusion.1
  524.9 2.0 convolution_convert_fusion.1
  526.9 1.4 copy.35
  528.3 1.2 copy.37
  529.5 28.2 %all_to_all.10 = bf16[4,8,32,1024]{3,2,1,0:T(8,128)(2,1)S(1)} all-to-all(bf16[4,8,32,1024]{3,2,1,0:T(8,128)(2,1)S(1)} %bitcast.17), channel_id=1, replica_groups=mesh['dp'=4,'tensor'=8] {'dp'}, dimensions={0} | all-to-all | bytes 4194304 | tf_op jit(solution)/shard_map/all_to_all | solution.py:58
  557.7 1.5 copy.33
  559.1 4.3 all-to-all-start.1
  563.5 0.1 copy.30
  563.6 0.1 broadcast_add_fusion
  563.6 0.1 reshape.60
  563.7 8.3 %scatter_custom_fusion = s32[2048]{0:T(1024)S(1)} fusion(s32[2048]{0:T(1024)S(1)} %get-tuple-element.5, s32[2048]{0:T(1024)S(1)} %reshape.60, s32[]{:T(128)} %constant.62.clone.1), kind=kCustom, calls=%fused_computation.43 | custom fusion | bytes 8196 | tf_op jit(solution)/shard_map/scatter | solution.py:66
  572.0 0.1 compare_and_fusion
  572.1 64.3 %all-to-all-done.1 = bf16[4,8,32,1024]{3,2,0,1:T(8,128)(2,1)} async-done(((bf16[4,8,32,1024]{3,2,0,1:T(8,128)(2,1)}), bf16[4,8,32,1024]{3,2,0,1:T(8,128)(2,1)}, u32[]{:S(2)}, u32[]{:S(2)}) %all-to-all-start.1) | async-done | bytes 2097184 | tf_op jit(solution)/shard_map/all_to_all | solution.py:57
  636.5 1.8 copy.34
  638.3 2.8 gather_fusion
  641.1 0.0 copy-start.4
  641.1 73.8 %all-reduce.2.cloned.1.call-done = bf16[512,4096]{1,0:T(8,128)(2,1)} async-done(((bf16[512,4096]{1,0:T(8,128)(2,1)}), bf16[512,4096]{1,0:T(8,128)(2,1)}) %all-reduce.2.cloned.1.call-update) | async-done | bytes 4194320 | tf_op jit(solution)/shard_map/psum | solution.py:86
  714.9 5.0 fusion.3
  719.9 0.0 copy-start.2
  719.9 1.9 copy-done.2
  721.8 0.8 constant_dynamic-slice_fusion
  722.7 51.0 %all-gather.14.cloned.1.call-done = bf16[4096,1024]{1,0:T(8,128)(2,1)} async-done(((bf16[1024,1024]{1,0:T(8,128)(2,1)}), bf16[4096,1024]{1,0:T(8,128)(2,1)}) %all-gather.14.cloned.1.call-update) | async-done | bytes 8388624 | tf_op jit(solution)/shard_map/all_gather | solution.py:92
  773.7 0.0 copy-done.4
  773.7 10.6 %multiply_reduce_fusion = (f32[512]{0:T(512)S(1)}, f32[512,1024]{1,0:T(8,128)}) fusion(bf16[512,1024]{1,0:T(8,128)(2,1)S(1)} %copy-done.4, pred[512]{0:T(512)(128)(4,1)S(1)} %get-tuple-element.3, bf16[512,4096]{1,0:T(8,128)(2,1)} %copy-done.2, bf16[4096,1024]{1,0:T(8,128)(2,1)} %all-gather.14.cloned.1.call-done), kind=kOutput, calls=%fused_computation.14 | convolution fusion | flops 4297588224 | bytes 15731200 | tf_op jit(solution)/shard_map/dot_general | solution.py:91
  784.3 21.3 %psum.15 = f32[512]{0:T(512)S(1)} all-reduce(f32[512]{0:T(512)S(1)} %get-tuple-element.7), channel_id=1, replica_groups=mesh['dp'=4,'tensor'=8] {'tensor'}, use_global_device_ids=true, to_apply=%region_8.9 | all-reduce | flops 512 | bytes 4096 | tf_op jit(solution)/shard_map/psum | solution.py:96
  805.6 0.6 broadcast_multiply_fusion
  806.2 0.0 copy-done.1
  (8 shorter events, 0.0 us)
Async XLA Ops:
  7.2 2.9 copy-start
  7.2 80.2 %all-gather.6.cloned.1.call-start = ((), (), s32[]{:S(2)}) async-start(), calls=%async_computation.3 | async-start | bytes 4718592 | tf_op jit(solution)/shard_map/all_gather | solution.py:69
  7.9 173.3 %all-gather.8.cloned.1.call-start = ((), (), s32[]{:S(2)}) async-start(), calls=%async_computation.4 | async-start | bytes 18350080 | tf_op jit(solution)/shard_map/all_gather | solution.py:79
  8.7 268.1 %all-gather.12.cloned.1.call-start = ((), (), s32[]{:S(2)}) async-start(), calls=%async_computation.6 | async-start | bytes 18350080 | tf_op jit(solution)/shard_map/all_gather | solution.py:83
  9.4 362.8 %all-gather.10.cloned.1.call-start = ((), (), s32[]{:S(2)}) async-start(), calls=%async_computation.5 | async-start | bytes 18350080 | tf_op jit(solution)/shard_map/all_gather | solution.py:80
  10.0 513.2 %reduce-scatter.2.cloned.1.call-start = ((), (), s32[]{:S(2)}) async-start(), calls=%async_computation.9 | async-start | bytes 9437184 | tf_op jit(solution)/shard_map/reduce_scatter | solution.py:27
  26.8 0.7 copy-start.6
  26.8 688.0 %all-reduce.2.cloned.1.call-start = ((), (), s32[]{:S(2)}) async-start(), calls=%async_computation.7 | async-start | bytes 8388608 | tf_op jit(solution)/shard_map/psum | solution.py:86
  401.0 0.8 copy-start.5
  401.0 0.8 copy-start.7
  401.0 122.2 %copy-start.3 = (bf16[64,8192]{1,0:T(8,128)(2,1)S(1)}, bf16[64,8192]{1,0:T(8,128)(2,1)}, u32[]{:S(2)}) copy-start(bf16[64,8192]{1,0:T(8,128)(2,1)} %param.13) | copy-start | bytes 3145732
  401.0 372.7 %all-gather.14.cloned.1.call-start = ((), (), s32[]{:S(2)}) async-start(), calls=%async_computation.8 | async-start | bytes 10485760 | tf_op jit(solution)/shard_map/all_gather | solution.py:92
  559.1 77.3 %all-to-all-start.1 = ((bf16[4,8,32,1024]{3,2,0,1:T(8,128)(2,1)}), bf16[4,8,32,1024]{3,2,0,1:T(8,128)(2,1)}, u32[]{:S(2)}, u32[]{:S(2)}) async-start(bf16[4,8,32,1024]{3,2,0,1:T(8,128)(2,1)} %copy.33), calls=%async_computation.2 | async-start | bytes 4194304 | tf_op jit(solution)/shard_map/all_to_all | solution.py:57
  641.1 132.7 %copy-start.4 = (bf16[512,1024]{1,0:T(8,128)(2,1)S(1)}, bf16[512,1024]{1,0:T(8,128)(2,1)}, u32[]{:S(2)}) copy-start(bf16[512,1024]{1,0:T(8,128)(2,1)} %gather_fusion) | copy-start | bytes 3145732
  719.9 2.0 copy-start.2
  773.7 32.5 %copy-start.1 = (bf16[512,1024]{1,0:T(8,128)(2,1)S(1)}, bf16[512,1024]{1,0:T(8,128)(2,1)}, u32[]{:S(2)}) copy-start(bf16[512,1024]{1,0:T(8,128)(2,1)} %param.11) | copy-start | bytes 3145732
Sparse Core Ops, SparseCore 0:
  10.0 77.3 all-gather.5
  89.0 92.1 all-gather.7
  182.8 93.9 all-gather.11
  278.2 93.9 all-gather.9
  375.7 147.4 reduce-scatter.1
  526.7 188.0 all-reduce.1
  716.4 57.2 all-gather.13
where the time goes:
time: 814 us; the launch traced here: 813 us
  waiting for transfers between devices  639 us (79%)
  matrix products  72.8 us (9%)
  blocking collectives  49.5 us (6%)
  local copies, waits for them, and re-layouts  20.5 us (3%)
  between operations  14.3 us (2%)
  other arithmetic  12.4 us (2%)
    reduce_scatter x1, waiting for transfers between devices, local(): lax.psum_scatter(jnp.dot(portion, w_out, preferred_element_type=jnp.float...  119 us
    all_gather x1, waiting for transfers between devices, local(): up_acts = add_rows(lax.all_gather(w_up, 'dp', axis=0, tiled=True))  95.4 us
    all_gather x1, waiting for transfers between devices, local(): gate_acts = add_rows(lax.all_gather(w_gate, 'dp', axis=0, tiled=True))  90.7 us
    all_gather x1, waiting for transfers between devices, local(): lax.all_gather(w_down, 'dp', axis=1, tiled=True)  80.9 us
    psum x1, waiting for transfers between devices, local(): lax.psum(partial_sum.astype(jnp.bfloat16), 'tensor').astype(jnp.float32)  73.8 us
    all_to_all x1, waiting for transfers between devices, local(): lax.all_to_all(lax.all_to_all(send_blocks, 'dp', split_axis=0, concat_axi...  64.3 us
    all_gather x1, waiting for transfers between devices, local(): gathered = lax.all_gather(student_in, 'tensor', axis=1, tiled=True)  59.9 us
    all_gather x1, waiting for transfers between devices, local(): lax.all_gather(proj, 'dp', axis=0, tiled=True)  51 us
  transfers between devices with their start and end apart: 8, of which 8 were waited for; matrix products, arithmetic and copies ran while one was open for 11% of the time, Pallas kernels for 0%

commit v1 on v0

--- a/solution.py
+++ b/solution.py
@@ -4,6 +4,10 @@
 from jax.sharding import PartitionSpec as P
 
 HT = 8192
+roots_render = lambda local_block: jnp.concatenate(
+    lax.all_to_all(jnp.stack(jnp.split(local_block, lax.axis_size("tensor"), 1)), "tensor", 0, 0),
+    axis=1,
+)
 
 
 def local(
@@ -54,12 +58,8 @@
     send_blocks = packed.reshape(group_count, capacity, tensor_count, col_width).transpose(
         0, 2, 1, 3
     )
-    arrived = lax.all_to_all(
-        lax.all_to_all(send_blocks, "dp", split_axis=0, concat_axis=0, tiled=True),
-        "tensor",
-        split_axis=1,
-        concat_axis=1,
-        tiled=True,
+    arrived = roots_render(
+        lax.all_to_all(send_blocks, "dp", split_axis=0, concat_axis=0, tiled=True)
     )
     flattened = arrived.reshape(source_count * capacity, col_width)
     arrival_index = (jnp.arange(source_count)[:, None] * capacity + slot_index).reshape(-1)

time: 814 us -> 812 us (level)
  transfers between devices with their start and end apart: 8 -> 8, of which waited for: 8 -> 8; matrix products, arithmetic and copies ran while one was open for 11% -> 12% of each run, Pallas kernels for 0% -> 0%
where the time goes in v1:
time: 812 us
  waiting for transfers between devices  632 us (78%)
  matrix products  72.9 us (9%)
  blocking collectives  49.5 us (6%)
  local copies, waits for them, and re-layouts  26.1 us (3%)
  between operations  14.3 us (2%)
  other arithmetic  12.4 us (2%)
    reduce_scatter x1, waiting for transfers between devices, local(): lax.psum_scatter(jnp.dot(portion, w_out, preferred_element_type=jnp.float...  119 us
    all_gather x1, waiting for transfers between devices, local(): up_acts = add_rows(lax.all_gather(w_up, 'dp', axis=0, tiled=True))  95.4 us
    all_gather x1, waiting for transfers between devices, local(): gate_acts = add_rows(lax.all_gather(w_gate, 'dp', axis=0, tiled=True))  90.7 us
    all_gather x1, waiting for transfers between devices, local(): lax.all_gather(w_down, 'dp', axis=1, tiled=True)  80.8 us
    psum x1, waiting for transfers between devices, local(): lax.psum(partial_sum.astype(jnp.bfloat16), 'tensor').astype(jnp.float32)  71.1 us
    all_to_all x1, waiting for transfers between devices, lax.all_to_all(jnp.stack(jnp.split(local_block, lax.axis_size('tensor'),...  60.6 us
    all_gather x1, waiting for transfers between devices, local(): gathered = lax.all_gather(student_in, 'tensor', axis=1, tiled=True)  59.9 us
    all_gather x1, waiting for transfers between devices, local(): lax.all_gather(proj, 'dp', axis=0, tiled=True)  51 us
  transfers between devices with their start and end apart: 8, of which 8 were waited for; matrix products, arithmetic and copies ran while one was open for 12% of the time, Pallas kernels for 0%

profile of v1, /device:TPU:0, one launch (start us, length us, event | category | flops | bytes accessed | tf_op | source)
XLA Modules:
  0.0 811.6 jit_solution(995015661077062070)
XLA Ops:
  7.2 0.0 copy-start
  7.2 0.0 all-gather.6.cloned.1.call-start
  7.2 0.7 all-gather.6.cloned.1.call-update
  7.9 0.0 all-gather.8.cloned.1.call-start
  8.0 0.7 all-gather.8.cloned.1.call-update
  8.7 0.0 all-gather.12.cloned.1.call-start
  8.7 0.7 all-gather.12.cloned.1.call-update
  9.4 0.0 all-gather.10.cloned.1.call-start
  9.4 0.5 all-gather.10.cloned.1.call-update
  10.0 0.0 reduce-scatter.2.cloned.1.call-start
  10.0 0.0 copy-done
  10.0 16.8 %convolution_convert_fusion = bf16[512,8192]{1,0:T(8,128)(2,1)} fusion(bf16[512,1024]{1,0:T(8,128)(2,1)S(1)} %copy-done, bf16[1024,8192]{1,0:T(8,128)(2,1)} %param.12), kind=kOutput, calls=%fused_computation.5 | convolution fusion | flops 8594128896 | bytes 26214400 | tf_op jit(solution)/shard_map/dot_general | solution.py:32
  26.8 0.0 reduce-scatter.2.cloned.1.call-update
  26.9 0.2 all-reduce.2.cloned.1.call-start
  27.1 0.4 copy-done.7
  27.5 59.9 %all-gather.6.cloned.1.call-done = bf16[512,4096]{1,0:T(8,128)(2,1)} async-done(((bf16[512,512]{1,0:T(8,128)(2,1)}), bf16[512,4096]{1,0:T(8,128)(2,1)}) %all-gather.6.cloned.1.call-update) | async-done | bytes 4194320 | tf_op jit(solution)/shard_map/all_gather | solution.py:69
  87.4 3.1 fusion
  90.5 90.7 %all-gather.8.cloned.1.call-done = bf16[4096,1792]{1,0:T(8,128)(2,1)} async-done(((bf16[1024,1792]{1,0:T(8,128)(2,1)}), bf16[4096,1792]{1,0:T(8,128)(2,1)}) %all-gather.8.cloned.1.call-update) | async-done | bytes 14680080 | tf_op jit(solution)/shard_map/all_gather | solution.py:79
  181.2 14.8 %fusion.11 = f32[512,1792]{1,0:T(8,128)} fusion(bf16[4096,1792]{1,0:T(8,128)(2,1)} %all-gather.8.cloned.1.call-done, bf16[512,4096]{1,0:T(8,128)(2,1)} %all-gather.6.cloned.1.call-done, f32[4096]{0:T(1024)S(1)} %convert_element_type.47, f32[512]{0:T(512)S(1)} %add_rsqrt_fusion), kind=kOutput, calls=%fused_computation.23 | convolution fusion | flops 7524581376 | bytes 22562816 | tf_op jit(solution)/shard_map/dot_general | solution.py:77
  195.9 80.8 %all-gather.12.cloned.1.call-done = bf16[1792,4096]{1,0:T(8,128)(2,1)} async-done(((bf16[1792,1024]{1,0:T(8,128)(2,1)}), bf16[1792,4096]{1,0:T(8,128)(2,1)}) %all-gather.12.cloned.1.call-update) | async-done | bytes 14680080 | tf_op jit(solution)/shard_map/all_gather | solution.py:83
  276.8 95.4 %all-gather.10.cloned.1.call-done = bf16[4096,1792]{1,0:T(8,128)(2,1)} async-done(((bf16[1024,1792]{1,0:T(8,128)(2,1)}), bf16[4096,1792]{1,0:T(8,128)(2,1)}) %all-gather.10.cloned.1.call-update) | async-done | bytes 14680080 | tf_op jit(solution)/shard_map/all_gather | solution.py:80
  372.2 28.8 %convolution_convert_fusion.2 = bf16[512,4096]{1,0:T(8,128)(2,1)} fusion(bf16[1792,4096]{1,0:T(8,128)(2,1)} %all-gather.12.cloned.1.call-done, f32[512,1792]{1,0:T(8,128)} %fusion.11, bf16[4096,1792]{1,0:T(8,128)(2,1)} %all-gather.10.cloned.1.call-done, bf16[512,4096]{1,0:T(8,128)(2,1)} %all-gather.6.cloned.1.call-done, f32[4096]{0:T(1024)S(1)} %convert_element_type.47, ...), kind=kOutput, calls=%fused_computation.11 | convolution fusion | flops 15048376320 | bytes 41437184 | tf_op jit(solution)/shard_map/dot_general | solution.py:82
  401.0 0.0 all-reduce.2.cloned.1.call-update
  401.0 0.3 all-gather.14.cloned.1.call-start
  401.3 0.5 all-gather.14.cloned.1.call-update
  401.8 0.0 copy-done.6
  401.8 0.0 copy-done.8
  401.8 0.1 eq.30
  401.9 0.1 copy.49
  402.0 1.7 select_reduce_fusion
  403.7 0.2 add_reduce_fusion
  403.9 119.3 %reduce-scatter.2.cloned.1.call-done = bf16[64,8192]{1,0:T(8,128)(2,1)} async-done(((bf16[512,8192]{1,0:T(8,128)(2,1)}), bf16[64,8192]{1,0:T(8,128)(2,1)}) %reduce-scatter.2.cloned.1.call-update) | async-done | bytes 1048592 | tf_op jit(solution)/shard_map/reduce_scatter | solution.py:31
  523.2 1.7 multiply_reduce_fusion.1
  524.9 2.0 convolution_convert_fusion.1
  526.9 1.4 copy.70
  528.3 1.2 copy.72
  529.4 28.2 %all_to_all.10 = bf16[4,8,32,1024]{3,2,1,0:T(8,128)(2,1)S(1)} all-to-all(bf16[4,8,32,1024]{3,2,1,0:T(8,128)(2,1)S(1)} %bitcast.67), channel_id=1, replica_groups=mesh['dp'=4,'tensor'=8] {'dp'}, dimensions={0} | all-to-all | bytes 4194304 | tf_op jit(solution)/shard_map/all_to_all | solution.py:62
  557.6 0.7 fusion.23
  558.4 0.7 fusion.22
  559.1 0.7 fusion.21
  559.8 0.7 fusion.20
  560.5 0.7 fusion.19
  561.2 0.7 fusion.18
  562.0 0.7 fusion.17
  562.7 0.7 fusion.16
  563.4 3.7 all-to-all-start.1
  567.1 0.1 copy.50
  567.2 0.1 broadcast_add_fusion
  567.3 0.1 reshape.60
  567.3 8.3 %scatter_custom_fusion = s32[2048]{0:T(1024)S(1)} fusion(s32[2048]{0:T(1024)S(1)} %get-tuple-element.5, s32[2048]{0:T(1024)S(1)} %reshape.60, s32[]{:T(128)} %constant.62.clone.1), kind=kCustom, calls=%fused_computation.59 | custom fusion | bytes 8196 | tf_op jit(solution)/shard_map/scatter | solution.py:66
  575.7 0.1 compare_and_fusion
  575.8 60.6 %all-to-all-done.1 = bf16[8,4,1,32,1024]{4,3,1,2,0:T(8,128)(2,1)S(1)} async-done(((bf16[8,4,1,32,1024]{4,3,1,2,0:T(8,128)(2,1)}), bf16[8,4,1,32,1024]{4,3,1,2,0:T(8,128)(2,1)S(1)}, u32[]{:S(2)}, u32[]{:S(2)}) %all-to-all-start.1) | async-done | bytes 2097184 | tf_op jit(solution)/shard_map/all_to_all | solution.py:8
  636.4 1.3 copy-done.2
  637.7 1.8 copy.61
  639.5 2.8 gather_fusion
  642.3 71.1 %all-reduce.2.cloned.1.call-done = bf16[512,4096]{1,0:T(8,128)(2,1)} async-done(((bf16[512,4096]{1,0:T(8,128)(2,1)}), bf16[512,4096]{1,0:T(8,128)(2,1)}) %all-reduce.2.cloned.1.call-update) | async-done | bytes 4194320 | tf_op jit(solution)/shard_map/psum | solution.py:86
  713.4 5.0 fusion.3
  718.4 2.0 copy-done.3
  720.4 0.8 constant_dynamic-slice_fusion
  721.2 51.0 %all-gather.14.cloned.1.call-done = bf16[4096,1024]{1,0:T(8,128)(2,1)} async-done(((bf16[1024,1024]{1,0:T(8,128)(2,1)}), bf16[4096,1024]{1,0:T(8,128)(2,1)}) %all-gather.14.cloned.1.call-update) | async-done | bytes 8388624 | tf_op jit(solution)/shard_map/all_gather | solution.py:92
  772.2 0.0 copy-done.5
  772.2 10.6 %multiply_reduce_fusion = (f32[512]{0:T(512)S(1)}, f32[512,1024]{1,0:T(8,128)}) fusion(bf16[512,1024]{1,0:T(8,128)(2,1)S(1)} %copy-done.5, pred[512]{0:T(512)(128)(4,1)S(1)} %get-tuple-element.3, bf16[512,4096]{1,0:T(8,128)(2,1)} %copy-done.3, bf16[4096,1024]{1,0:T(8,128)(2,1)} %all-gather.14.cloned.1.call-done), kind=kOutput, calls=%fused_computation.14 | convolution fusion | flops 4297588224 | bytes 15731200 | tf_op jit(solution)/shard_map/dot_general | solution.py:91
  782.8 21.3 %psum.15 = f32[512]{0:T(512)S(1)} all-reduce(f32[512]{0:T(512)S(1)} %get-tuple-element.7), channel_id=1, replica_groups=mesh['dp'=4,'tensor'=8] {'tensor'}, use_global_device_ids=true, to_apply=%region_8.9 | all-reduce | flops 512 | bytes 4096 | tf_op jit(solution)/shard_map/psum | solution.py:96
  804.2 0.6 broadcast_multiply_fusion
  (17 shorter events, 0.1 us)
Async XLA Ops:
  7.2 2.9 copy-start
  7.2 80.2 %all-gather.6.cloned.1.call-start = ((), (), s32[]{:S(2)}) async-start(), calls=%async_computation.3 | async-start | bytes 4718592 | tf_op jit(solution)/shard_map/all_gather | solution.py:69
  7.9 173.3 %all-gather.8.cloned.1.call-start = ((), (), s32[]{:S(2)}) async-start(), calls=%async_computation.4 | async-start | bytes 18350080 | tf_op jit(solution)/shard_map/all_gather | solution.py:79
  8.7 268.1 %all-gather.12.cloned.1.call-start = ((), (), s32[]{:S(2)}) async-start(), calls=%async_computation.6 | async-start | bytes 18350080 | tf_op jit(solution)/shard_map/all_gather | solution.py:83
  9.4 362.8 %all-gather.10.cloned.1.call-start = ((), (), s32[]{:S(2)}) async-start(), calls=%async_computation.5 | async-start | bytes 18350080 | tf_op jit(solution)/shard_map/all_gather | solution.py:80
  10.0 513.2 %reduce-scatter.2.cloned.1.call-start = ((), (), s32[]{:S(2)}) async-start(), calls=%async_computation.9 | async-start | bytes 9437184 | tf_op jit(solution)/shard_map/reduce_scatter | solution.py:31
  26.8 0.7 copy-start.7
  26.9 686.5 %all-reduce.2.cloned.1.call-start = ((), (), s32[]{:S(2)}) async-start(), calls=%async_computation.7 | async-start | bytes 8388608 | tf_op jit(solution)/shard_map/psum | solution.py:86
  401.0 0.8 copy-start.6
  401.0 0.8 copy-start.8
  401.0 122.2 %copy-start.4 = (bf16[64,8192]{1,0:T(8,128)(2,1)S(1)}, bf16[64,8192]{1,0:T(8,128)(2,1)}, u32[]{:S(2)}) copy-start(bf16[64,8192]{1,0:T(8,128)(2,1)} %param.13) | copy-start | bytes 3145732
  401.0 371.2 %all-gather.14.cloned.1.call-start = ((), (), s32[]{:S(2)}) async-start(), calls=%async_computation.8 | async-start | bytes 10485760 | tf_op jit(solution)/shard_map/all_gather | solution.py:92
  563.4 73.0 %all-to-all-start.1 = ((bf16[8,4,1,32,1024]{4,3,1,2,0:T(8,128)(2,1)}), bf16[8,4,1,32,1024]{4,3,1,2,0:T(8,128)(2,1)S(1)}, u32[]{:S(2)}, u32[]{:S(2)}) async-start(bf16[8,4,1,32,1024]{4,3,1,2,0:T(8,128)(2,1)} %fusion.16), calls=%async_computation.2 | async-start | bytes 4194304 | tf_op jit(solution)/shard_map/all_to_all | solution.py:8
  636.4 1.3 copy-start.2
  642.3 129.9 %copy-start.5 = (bf16[512,1024]{1,0:T(8,128)(2,1)S(1)}, bf16[512,1024]{1,0:T(8,128)(2,1)}, u32[]{:S(2)}) copy-start(bf16[512,1024]{1,0:T(8,128)(2,1)} %gather_fusion) | copy-start | bytes 3145732
  718.4 2.0 copy-start.3
  772.2 32.5 %copy-start.1 = (bf16[512,1024]{1,0:T(8,128)(2,1)S(1)}, bf16[512,1024]{1,0:T(8,128)(2,1)}, u32[]{:S(2)}) copy-start(bf16[512,1024]{1,0:T(8,128)(2,1)} %param.11) | copy-start | bytes 3145732
Sparse Core Ops, SparseCore 0:
  10.0 77.3 all-gather.5
  89.0 92.1 all-gather.7
  182.7 93.9 all-gather.11
  278.2 93.9 all-gather.9
  375.7 147.4 reduce-scatter.1
  526.7 186.6 all-reduce.1
  714.9 57.2 all-gather.13
